TPU v7x, 32 devices: a whole 2x2x4 slice. The times are simulated.
32 devices in a mesh: days: 4 (over y, x), space: 8 (over z, core).
Axes of the slice: x: 2, y: 2, z: 4, core: 2. Of those that a mesh axis runs over, the one named last changes fastest.
Arguments:
- fields: bfloat16 [640, 32, 1440], P('days', 'space')
- month_label: int32 [640], P('days'), may hold values from 0 to 11, as said below
- row_index: int32 [32], P('space'), may hold values from 0 to 31
- area_table: float32 [32], replicated, may hold values from 0.05 to 1
- basis: bfloat16 [64, 32, 1440], P(None, 'space'), may hold values from -6 to 6
Outputs:
- eofs: float32 [64, 32, 1440], P(None, 'space')
- pcs: float32 [640, 64], P('days')
Inputs may be any that keep to these rules, and one draw needn't show every extreme that they name: `month_label`: each day's label differs from floor(12 * day / 640) by at most one; the first day with a given value of floor(12 * day / 640) carries exactly that value; every month labels at least one day.
All inputs are finite; a program needn't handle non-finite values.
Results may differ from a plain program's by a relative error of at most 0.0003.
Values sent between devices are 32-bit elements; how exact they have to be, the bound alone decides.
A program may use at most 64 MiB of HBM per device.

v0:
```python
import jax
import jax.numpy as jnp
from jax import lax
from jax.sharding import PartitionSpec as P

ITERS = 2
HIGH = lax.Precision.HIGHEST


def solve_lower(lower, cover):
    shape = cover.shape
    solved = lax.linalg.triangular_solve(
        lower, cover.reshape(shape[0], -1), left_side=True, lower=True
    )
    return solved.reshape(shape)


def self_gram(cover):
    return jnp.einsum("klc,jlc->kj", cover, cover, precision=HIGH)


def local(fields, month_label, row_index, area_table, basis):
    months = jnp.arange(12, dtype=jnp.int32)
    onehot = (month_label[None, :] == months[:, None]).astype(jnp.bfloat16)
    sums = jnp.einsum("md,dlc->mlc", onehot, fields, preferred_element_type=jnp.float32)
    counts = jnp.sum(onehot.astype(jnp.float32), axis=1)
    sums, counts = lax.psum((sums, counts), "days")
    climate = sums / counts[:, None, None]
    seasonal = jnp.einsum("md,mlc->dlc", onehot.astype(jnp.float32), climate, precision=HIGH)
    table_hot = (
        row_index[:, None] == jnp.arange(area_table.shape[0], dtype=jnp.int32)[None, :]
    ).astype(jnp.float32)
    scale = jnp.sqrt(jnp.dot(table_hot, area_table, precision=HIGH))
    weighted = (fields.astype(jnp.float32) - seasonal) * scale[None, :, None]
    days_total = fields.shape[0] * lax.axis_size("days")
    partial_pcs = jnp.einsum("dlc,klc->dk", weighted, basis.astype(jnp.float32), precision=HIGH)
    pcs = lax.psum(partial_pcs, "space")
    eofs = basis.astype(jnp.float32)
    for step_count in range(ITERS):
        partial_cover = jnp.einsum("dk,dlc->klc", pcs, weighted, precision=HIGH) / days_total
        cover = lax.psum(partial_cover, "days")
        partial_gram = self_gram(cover)
        partial_raw = jnp.einsum("dlc,klc->dk", weighted, cover, precision=HIGH)
        gram, raw_pcs = lax.psum((partial_gram, partial_raw), "space")
        lower = jnp.linalg.cholesky(gram)
        eofs = solve_lower(lower, cover)
        pcs = lax.linalg.triangular_solve(
            lower, raw_pcs, left_side=False, lower=True, transpose_a=True
        )
    return (eofs, pcs)


def solution(mesh):
    placed = (P("days", "space", None), P("days"), P("space"), P(), P(None, "space", None))
    return jax.shard_map(
        local,
        mesh=mesh,
        in_specs=placed,
        out_specs=(P(None, "space", None), P("days", None)),
        check_vma=False,
    )
```

profile of v0, /device:TPU:0, one launch (start us, length us, event | category | flops | bytes accessed | tf_op | source)
XLA Modules:
  0.0 343.0 jit_solution(18154794807191105921)
XLA Ops:
  7.3 3.1 fusion
  10.6 11.5 %psum.64 = f32[12]{0:T(128)S(1)} all-reduce(f32[12]{0:T(128)S(1)} %convert_reduce_fusion), channel_id=1, replica_groups=mesh['days'=4,'space'=8] {'days'}, use_global_device_ids=true, to_apply=%region_2.0 | all-reduce | flops 12 | bytes 96 | tf_op jit(solution)/shard_map/psum | solution.py:27
  22.2 36.2 %all-reduce.6.cloned.1.call-done = f32[12,4,1440]{2,0,1:T(8,128)} async-done(((f32[12,4,1440]{2,0,1:T(8,128)}), f32[12,4,1440]{2,0,1:T(8,128)}) %all-reduce.6.cloned.1.call-update) | async-done | bytes 276496 | tf_op jit(solution)/shard_map/psum | solution.py:27
  58.4 3.2 subtract_multiply_fusion
  63.5 2.4 convolution_bitcast_fusion.4
  65.9 28.5 %psum.65 = f32[160,64]{0,1:T(8,128)S(1)} all-reduce(f32[160,64]{0,1:T(8,128)S(1)} %convolution_bitcast_fusion.4), channel_id=1, replica_groups=mesh['days'=4,'space'=8] {'space'}, use_global_device_ids=true, to_apply=%region_3.0 | all-reduce | flops 10240 | bytes 81920 | tf_op jit(solution)/shard_map/psum | solution.py:37
  94.4 5.4 %convolution_multiply_fusion.1 = f32[64,4,1440]{2,0,1:T(8,128)} fusion(f32[160,4,1440]{2,0,1:T(8,128)} %copy-done.1, f32[160,64]{0,1:T(8,128)S(1)} %psum.65), kind=kOutput, calls=%fused_computation.2 | convolution fusion | flops 708157440 | bytes 5201920 | tf_op jit(solution)/shard_map/dk,dlc->klc/dot_general | solution.py:40
  100.1 57.9 %all-reduce.8.cloned.1.call-done = f32[64,4,1440]{2,0,1:T(8,128)} async-done(((f32[64,4,1440]{2,0,1:T(8,128)}), f32[64,4,1440]{2,0,1:T(8,128)}) %all-reduce.8.cloned.1.call-update) | async-done | bytes 1474576 | tf_op jit(solution)/shard_map/psum | solution.py:41
  157.9 3.5 %convolution_bitcast_fusion.6 = f32[64,64]{0,1:T(8,128)S(1)} fusion(f32[64,4,1440]{2,0,1:T(8,128)} %all-reduce.8.cloned.1.call-done), kind=kOutput, calls=%fused_computation.13 | convolution fusion | flops 283115520 | bytes 1490944 | tf_op jit(solution)/shard_map/klc,jlc->kj/dot_general | solution.py:19
  161.4 5.3 %convolution_bitcast_fusion.1 = f32[160,64]{1,0:T(8,128)S(1)} fusion(f32[160,4,1440]{2,0,1:T(8,128)} %copy-done.1, f32[64,4,1440]{2,0,1:T(8,128)S(1)} %copy-done.3), kind=kOutput, calls=%fused_computation.8 | convolution fusion | flops 707788800 | bytes 5201920 | tf_op jit(solution)/shard_map/dlc,klc->dk/dot_general | solution.py:43
  166.7 29.8 %all-reduce.1 = (f32[160,64]{1,0:T(8,128)S(1)}, f32[64,64]{0,1:T(8,128)S(1)}) all-reduce(f32[160,64]{1,0:T(8,128)S(1)} %convolution_bitcast_fusion.1, f32[64,64]{0,1:T(8,128)S(1)} %convolution_bitcast_fusion.6), channel_id=1, replica_groups=mesh['days'=4,'space'=8] {'space'}, use_global_device_ids=true, to_apply=%region_8.0 | all-reduce | flops 14336 | bytes 114688 | tf_op jit(solution)/shard_map/psum | solution.py:44
  196.7 5.8 %cholesky.44 = f32[64,64]{1,0:T(8,128)S(1)} custom-call(f32[64,64]{1,0:T(8,128)S(1)} %fusion.15), custom_call_target="Cholesky" | custom-call | tf_op jit(solution)/shard_map/jit(cholesky)/cholesky | solution.py:45
  203.8 4.9 %custom-call.10 = f32[1,64,64]{1,2,0:T(8,128)S(1)} custom-call(f32[1,64,64]{2,1,0:T(8,128)S(1)} %fusion.9), custom_call_target="InvertDiagBlocksLowerTriangular" | custom-call | tf_op jit(solution)/shard_map/triangular_solve/custom-call.0 | solution.py:47
  209.1 5.4 %convolution_multiply_fusion = f32[64,4,1440]{2,0,1:T(8,128)} fusion(f32[160,64,1]{0,1,2:T(8,128)S(1)} %convolution_bitcast_fusion.3, f32[160,4,1440]{2,0,1:T(8,128)} %copy-done.1), kind=kOutput, calls=%fused_computation.1 | convolution fusion | flops 708157440 | bytes 5201920 | tf_op jit(solution)/shard_map/dk,dlc->klc/dot_general | solution.py:40
  214.5 58.1 %all-reduce.10.cloned.1.call-done = f32[64,4,1440]{2,0,1:T(8,128)} async-done(((f32[64,4,1440]{2,0,1:T(8,128)}), f32[64,4,1440]{2,0,1:T(8,128)}) %all-reduce.10.cloned.1.call-update) | async-done | bytes 1474576 | tf_op jit(solution)/shard_map/psum | solution.py:41
  272.6 3.6 %copy.19 = f32[64,4,1440]{2,1,0:T(4,128)} copy(f32[64,4,1440]{2,0,1:T(8,128)} %all-reduce.10.cloned.1.call-done) | data formatting | bytes 2949120 | tf_op jit(solution)/shard_map/psum | solution.py:41
  276.2 3.3 reshape.27
  279.5 5.3 %convolution_bitcast_fusion = f32[160,64]{1,0:T(8,128)S(1)} fusion(f32[160,4,1440]{2,0,1:T(8,128)} %copy-done.1, f32[64,4,1440]{2,0,1:T(8,128)S(1)} %copy-done.2), kind=kOutput, calls=%fused_computation.7 | convolution fusion | flops 707788800 | bytes 5201920 | tf_op jit(solution)/shard_map/dlc,klc->dk/dot_general | solution.py:43
  286.2 30.2 %all-reduce = (f32[64,64]{0,1:T(8,128)S(1)}, f32[160,64]{1,0:T(8,128)S(1)}) all-reduce(f32[64,64]{0,1:T(8,128)S(1)} %convolution_bitcast_fusion.5, f32[160,64]{1,0:T(8,128)S(1)} %convolution_bitcast_fusion), channel_id=1, replica_groups=mesh['days'=4,'space'=8] {'space'}, use_global_device_ids=true, to_apply=%region_10.13 | all-reduce | flops 14336 | bytes 114688 | tf_op jit(solution)/shard_map/psum | solution.py:44
  316.5 5.8 %cholesky.55 = f32[64,64]{1,0:T(8,128)S(1)} custom-call(f32[64,64]{1,0:T(8,128)S(1)} %fusion.13), custom_call_target="Cholesky" | custom-call | tf_op jit(solution)/shard_map/jit(cholesky)/cholesky | solution.py:45
  323.7 4.9 %custom-call.8 = f32[1,64,64]{1,2,0:T(8,128)S(1)} custom-call(f32[1,64,64]{2,1,0:T(8,128)S(1)} %fusion.10), custom_call_target="InvertDiagBlocksLowerTriangular" | custom-call | tf_op jit(solution)/shard_map/triangular_solve | solution.py:12
  328.6 2.9 triangular_solve.34
  332.5 1.9 fusion.2
  334.4 2.2 copy.22
  (37 shorter events, 8.0 us)
Async XLA Ops:
  7.2 56.3 %copy-start = (bf16[64,4,1440]{2,1,0:T(4,128)(2,1)S(1)}, bf16[64,4,1440]{2,1,0:T(4,128)(2,1)}, u32[]{:S(2)}) copy-start(bf16[64,4,1440]{2,1,0:T(4,128)(2,1)} %param.12) | copy-start | bytes 2211844
  7.2 3.3 copy-start.5
  7.2 51.2 %copy-start.4 = (bf16[160,4,1440]{2,1,0:T(4,128)(2,1)S(1)}, bf16[160,4,1440]{2,1,0:T(4,128)(2,1)}, u32[]{:S(2)}) copy-start(bf16[160,4,1440]{2,1,0:T(4,128)(2,1)} %param.8) | copy-start | bytes 5529604
  7.2 14.8 %copy-start.7 = (f32[32]{0:T(128)S(1)}, f32[32]{0:T(128)}, u32[]{:S(2)}) copy-start(f32[32]{0:T(128)} %param.11) | copy-start | bytes 388
  7.2 14.8 %copy-start.6 = (s32[4]{0:T(128)S(1)}, s32[4]{0:T(128)}, u32[]{:S(2)}) copy-start(s32[4]{0:T(128)} %param.10) | copy-start | bytes 52
  7.2 51.2 %all-reduce.6.cloned.1.call-start = ((), (), s32[]{:S(2)}) async-start(), calls=%async_computation | async-start | bytes 786432 | tf_op jit(solution)/shard_map/psum | solution.py:27
  10.4 147.5 %all-reduce.8.cloned.1.call-start = ((), (), s32[]{:S(2)}) async-start(), calls=%async_computation.1 | async-start | bytes 3145728 | tf_op jit(solution)/shard_map/psum | solution.py:41
  61.6 1.9 copy-start.1
  99.8 172.8 %all-reduce.10.cloned.1.call-start = ((), (), s32[]{:S(2)}) async-start(), calls=%async_computation.2 | async-start | bytes 3145728 | tf_op jit(solution)/shard_map/psum | solution.py:41
  157.9 3.5 %copy-start.3 = (f32[64,4,1440]{2,0,1:T(8,128)S(1)}, f32[64,4,1440]{2,0,1:T(8,128)}, u32[]{:S(2)}) copy-start(f32[64,4,1440]{2,0,1:T(8,128)} %all-reduce.8.cloned.1.call-done) | copy-start | bytes 4423684
  276.2 3.3 copy-start.2
Sparse Core Ops, SparseCore 0:
  11.6 46.8 all-reduce.5
  99.9 57.9 all-reduce.7
  214.6 57.9 all-reduce.9
where the time goes:
time: 343 us
  waiting for transfers between devices  152 us (44%)
  blocking collectives  100 us (29%)
  matrix products  38.3 us (11%)
  other arithmetic  24.3 us (7%)
  local copies, waits for them, and re-layouts  14 us (4%)
  between operations  13.9 us (4%)
    psum x2, waiting for transfers between devices, local(): cover = lax.psum(partial_cover, 'days')  116 us
    psum x2, blocking collectives, local(): gram, raw_pcs = lax.psum((partial_gram, partial_raw), 'space')  60 us
    psum x1, waiting for transfers between devices, local(): sums, counts = lax.psum((sums, counts), 'days')  36.2 us
    psum x1, blocking collectives, local(): pcs = lax.psum(partial_pcs, 'space')  28.5 us
    another operation x6, other arithmetic, local(): lower = jnp.linalg.cholesky(gram)  13 us
    psum x1, blocking collectives, local(): sums, counts = lax.psum((sums, counts), 'days')  11.5 us
    dot_general x2, matrix products, local(): jnp.einsum('dk,dlc->klc', pcs, weighted, precision=HIGH) / days_total  10.8 us
    dot_general x2, matrix products, local(): partial_raw = jnp.einsum('dlc,klc->dk', weighted, cover, precision=HIGH)  10.6 us
  transfers between devices with their start and end apart: 3, of which 3 were waited for; matrix products, arithmetic and copies ran while one was open for 0% of the time, Pallas kernels for 0%

commit v1 on v0

--- a/solution.py
+++ b/solution.py
@@ -38,7 +38,7 @@
     eofs = basis.astype(jnp.float32)
     for step_count in range(ITERS):
         partial_cover = jnp.einsum("dk,dlc->klc", pcs, weighted, precision=HIGH) / days_total
-        cover = lax.psum(partial_cover, "days")
+        cover = jnp.sum(lax.all_gather(partial_cover, "days"), axis=0)
         partial_gram = self_gram(cover)
         partial_raw = jnp.einsum("dlc,klc->dk", weighted, cover, precision=HIGH)
         gram, raw_pcs = lax.psum((partial_gram, partial_raw), "space")

time: 343 us -> 366 us (1.067)
  waiting for transfers between devices: 152 us -> 171 us
  other arithmetic: 24.3 us -> 31.5 us
    all_gather x0 -> x2, waiting for transfers between devices: none -> 135 us  [local(): cover = jnp.sum(lax.all_gather(partial_cover, 'days'), axis=0)]
    psum x2 -> x0, waiting for transfers between devices: 116 us -> none  [local(): cover = lax.psum(partial_cover, 'days')]
    reduce_sum x0 -> x2, other arithmetic: none -> 7.22 us  [local(): cover = jnp.sum(lax.all_gather(partial_cover, 'days'), axis=0)]
where the time goes in v1:
time: 366 us; the launch traced here: 365 us
  waiting for transfers between devices  171 us (47%)
  blocking collectives  98.9 us (27%)
  matrix products  37.6 us (10%)
  other arithmetic  31.5 us (9%)
  between operations  13.9 us (4%)
  local copies, waits for them, and re-layouts  12.5 us (3%)
    all_gather x2, waiting for transfers between devices, local(): cover = jnp.sum(lax.all_gather(partial_cover, 'days'), axis=0)  135 us
    psum x2, blocking collectives, local(): gram, raw_pcs = lax.psum((partial_gram, partial_raw), 'space')  58.9 us
    psum x1, waiting for transfers between devices, local(): sums, counts = lax.psum((sums, counts), 'days')  36.2 us
    psum x1, blocking collectives, local(): pcs = lax.psum(partial_pcs, 'space')  28.5 us
    another operation x6, other arithmetic, local(): lower = jnp.linalg.cholesky(gram)  13 us
    dot_general x2, matrix products, local(): partial_raw = jnp.einsum('dlc,klc->dk', weighted, cover, precision=HIGH)  12.1 us
    psum x1, blocking collectives, local(): sums, counts = lax.psum((sums, counts), 'days')  11.5 us
    dot_general x2, matrix products, local(): jnp.einsum('dk,dlc->klc', pcs, weighted, precision=HIGH) / days_total  10.8 us
  transfers between devices with their start and end apart: 3, of which 3 were waited for; matrix products, arithmetic and copies ran while one was open for 0% of the time, Pallas kernels for 0%

profile of v1, /device:TPU:0, one launch (start us, length us, event | category | flops | bytes accessed | tf_op | source)
XLA Modules:
  0.0 365.4 jit_solution(5898519945724968898)
XLA Ops:
  7.3 3.1 fusion
  10.6 11.5 %psum.50 = f32[12]{0:T(128)S(1)} all-reduce(f32[12]{0:T(128)S(1)} %convert_reduce_fusion), channel_id=1, replica_groups=mesh['days'=4,'space'=8] {'days'}, use_global_device_ids=true, to_apply=%region_2.0 | all-reduce | flops 12 | bytes 96 | tf_op jit(solution)/shard_map/psum | solution.py:27
  22.2 36.2 %all-reduce.4.cloned.1.call-done = f32[12,4,1440]{2,0,1:T(8,128)} async-done(((f32[12,4,1440]{2,0,1:T(8,128)}), f32[12,4,1440]{2,0,1:T(8,128)}) %all-reduce.4.cloned.1.call-update) | async-done | bytes 276496 | tf_op jit(solution)/shard_map/psum | solution.py:27
  58.4 3.2 subtract_multiply_fusion
  63.5 2.4 convolution_bitcast_fusion.4
  66.0 28.5 %psum.51 = f32[160,64]{0,1:T(8,128)S(1)} all-reduce(f32[160,64]{0,1:T(8,128)S(1)} %convolution_bitcast_fusion.4), channel_id=1, replica_groups=mesh['days'=4,'space'=8] {'space'}, use_global_device_ids=true, to_apply=%region_3.0 | all-reduce | flops 10240 | bytes 81920 | tf_op jit(solution)/shard_map/psum | solution.py:37
  94.5 5.4 %convolution_multiply_fusion.1 = f32[64,4,1440]{2,0,1:T(8,128)} fusion(f32[160,4,1440]{2,0,1:T(8,128)} %copy-done.1, f32[160,64]{0,1:T(8,128)S(1)} %psum.51), kind=kOutput, calls=%fused_computation.2 | convolution fusion | flops 708157440 | bytes 5201920 | tf_op jit(solution)/shard_map/dk,dlc->klc/dot_general | solution.py:40
  100.1 67.2 %all-gather.5.cloned.1.call-done = f32[256,4,1440]{2,0,1:T(8,128)} async-done(((f32[64,4,1440]{2,0,1:T(8,128)}), f32[256,4,1440]{2,0,1:T(8,128)}) %all-gather.5.cloned.1.call-update) | async-done | bytes 5898256 | tf_op jit(solution)/shard_map/all_gather | solution.py:41
  167.3 3.6 reduce_sum.28
  172.3 6.1 %convolution_bitcast_fusion.1 = f32[160,64]{0,1:T(8,128)S(1)} fusion(f32[160,4,1440]{2,0,1:T(8,128)} %copy-done.1, f32[64,4,1440]{2,0,1:T(8,128)S(1)} %reduce_sum.28), kind=kOutput, calls=%fused_computation.8 | convolution fusion | flops 707788800 | bytes 5201920 | tf_op jit(solution)/shard_map/dlc,klc->dk/dot_general | solution.py:43
  178.3 29.6 %all-reduce.1 = (f32[160,64]{0,1:T(8,128)S(1)}, f32[64,64]{0,1:T(8,128)S(1)}) all-reduce(f32[160,64]{0,1:T(8,128)S(1)} %convolution_bitcast_fusion.1, f32[64,64]{0,1:T(8,128)S(1)} %convolution_bitcast_fusion.6), channel_id=1, replica_groups=mesh['days'=4,'space'=8] {'space'}, use_global_device_ids=true, to_apply=%region_8.0 | all-reduce | flops 14336 | bytes 114688 | tf_op jit(solution)/shard_map/psum | solution.py:44
  208.0 5.8 %cholesky.44 = f32[64,64]{1,0:T(8,128)S(1)} custom-call(f32[64,64]{1,0:T(8,128)S(1)} %fusion.15), custom_call_target="Cholesky" | custom-call | tf_op jit(solution)/shard_map/jit(cholesky)/cholesky | solution.py:45
  215.2 4.9 %custom-call.10 = f32[1,64,64]{1,2,0:T(8,128)S(1)} custom-call(f32[1,64,64]{2,1,0:T(8,128)S(1)} %fusion.9), custom_call_target="InvertDiagBlocksLowerTriangular" | custom-call | tf_op jit(solution)/shard_map/triangular_solve/custom-call.0 | solution.py:47
  220.3 5.4 %convolution_multiply_fusion = f32[64,4,1440]{2,0,1:T(8,128)} fusion(f32[160,64,1]{0,1,2:T(8,128)S(1)} %convolution_bitcast_fusion.3, f32[160,4,1440]{2,0,1:T(8,128)} %copy-done.1), kind=kOutput, calls=%fused_computation.1 | convolution fusion | flops 708157440 | bytes 5201920 | tf_op jit(solution)/shard_map/dk,dlc->klc/dot_general | solution.py:40
  225.8 67.4 %all-gather.7.cloned.1.call-done = f32[256,4,1440]{2,0,1:T(8,128)} async-done(((f32[64,4,1440]{2,0,1:T(8,128)}), f32[256,4,1440]{2,0,1:T(8,128)}) %all-gather.7.cloned.1.call-update) | async-done | bytes 5898256 | tf_op jit(solution)/shard_map/all_gather | solution.py:41
  293.2 3.6 reduce_sum.29
  296.8 6.1 %convolution_bitcast_fusion = f32[160,64]{0,1:T(8,128)S(1)} fusion(f32[160,4,1440]{2,0,1:T(8,128)} %copy-done.1, f32[64,4,1440]{2,0,1:T(8,128)S(1)} %reduce_sum.29), kind=kOutput, calls=%fused_computation.7 | convolution fusion | flops 707788800 | bytes 5201920 | tf_op jit(solution)/shard_map/dlc,klc->dk/dot_general | solution.py:43
  304.2 2.2 copy.31
  306.4 3.2 reshape.27
  309.6 29.3 %all-reduce = (f32[64,64]{0,1:T(8,128)S(1)}, f32[160,64]{0,1:T(8,128)S(1)}) all-reduce(f32[64,64]{0,1:T(8,128)S(1)} %convolution_bitcast_fusion.5, f32[160,64]{0,1:T(8,128)S(1)} %convolution_bitcast_fusion), channel_id=1, replica_groups=mesh['days'=4,'space'=8] {'space'}, use_global_device_ids=true, to_apply=%region_10.13 | all-reduce | flops 14336 | bytes 114688 | tf_op jit(solution)/shard_map/psum | solution.py:44
  339.0 5.8 %cholesky.55 = f32[64,64]{1,0:T(8,128)S(1)} custom-call(f32[64,64]{1,0:T(8,128)S(1)} %fusion.13), custom_call_target="Cholesky" | custom-call | tf_op jit(solution)/shard_map/jit(cholesky)/cholesky | solution.py:45
  346.2 4.9 %custom-call.8 = f32[1,64,64]{1,2,0:T(8,128)S(1)} custom-call(f32[1,64,64]{2,1,0:T(8,128)S(1)} %fusion.10), custom_call_target="InvertDiagBlocksLowerTriangular" | custom-call | tf_op jit(solution)/shard_map/triangular_solve | solution.py:12
  351.1 2.9 triangular_solve.34
  356.8 2.2 copy.34
  (35 shorter events, 11.2 us)
Async XLA Ops:
  7.2 56.4 %copy-start = (bf16[64,4,1440]{2,1,0:T(4,128)(2,1)S(1)}, bf16[64,4,1440]{2,1,0:T(4,128)(2,1)}, u32[]{:S(2)}) copy-start(bf16[64,4,1440]{2,1,0:T(4,128)(2,1)} %param.12) | copy-start | bytes 2211844
  7.2 3.3 copy-start.3
  7.2 51.2 %copy-start.2 = (bf16[160,4,1440]{2,1,0:T(4,128)(2,1)S(1)}, bf16[160,4,1440]{2,1,0:T(4,128)(2,1)}, u32[]{:S(2)}) copy-start(bf16[160,4,1440]{2,1,0:T(4,128)(2,1)} %param.8) | copy-start | bytes 5529604
  7.2 14.8 %copy-start.5 = (f32[32]{0:T(128)S(1)}, f32[32]{0:T(128)}, u32[]{:S(2)}) copy-start(f32[32]{0:T(128)} %param.11) | copy-start | bytes 388
  7.2 14.8 %copy-start.4 = (s32[4]{0:T(128)S(1)}, s32[4]{0:T(128)}, u32[]{:S(2)}) copy-start(s32[4]{0:T(128)} %param.10) | copy-start | bytes 52
  7.2 51.2 %all-reduce.4.cloned.1.call-start = ((), (), s32[]{:S(2)}) async-start(), calls=%async_computation | async-start | bytes 786432 | tf_op jit(solution)/shard_map/psum | solution.py:27
  10.4 156.9 %all-gather.5.cloned.1.call-start = ((), (), s32[]{:S(2)}) async-start(), calls=%async_computation.1 | async-start | bytes 7864320 | tf_op jit(solution)/shard_map/all_gather | solution.py:41
  61.6 1.9 copy-start.1
  99.9 193.3 %all-gather.7.cloned.1.call-start = ((), (), s32[]{:S(2)}) async-start(), calls=%async_computation.2 | async-start | bytes 7864320 | tf_op jit(solution)/shard_map/all_gather | solution.py:41
Sparse Core Ops, SparseCore 0:
  11.6 46.8 all-reduce.3
  100.0 67.2 all-gather.4
  225.9 67.2 all-gather.6
